TPU v7x, 128 devices: a whole 4x4x4 slice. The times are simulated.
128 devices in a mesh: walk: 8 (over y, x_lo), orb: 16 (over x_hi, z, core).
Axes of the slice: x: 4 (x_hi: 2, x_lo: 2; x = x_hi * 2 + x_lo), y: 4, z: 4, core: 2. Of those that a mesh axis runs over, the one named last changes fastest.
Arguments:
- coefficients: bfloat16 [4096, 4096], P(None, 'orb'), may hold values from -6 to 6
- inverse: bfloat16 [8, 1024, 1024], P('walk', 'orb'), may hold values from -0.005859375 to 0.005859375
- cell_index: int32 [8, 3, 1024], P('walk'), may hold values from 0 to 15
- fraction: float32 [8, 3, 1024], P('walk'), may hold values from 0 to 1
- energies: float32 [8], P('walk'), may hold values from -8 to 8
- weights: float32 [8], P('walk'), may hold values from 0.5 to 2
- occupied: int32 [1024], replicated, may hold values from 0 to 4095, as said below
Outputs:
- gradient: float32 [1024, 4096], P('walk', 'orb')
Inputs may be any that keep to these rules, and one draw needn't show every extreme that they name: `occupied`: 1024 distinct orbital indices; every block of 256 consecutive orbital indices holds at most 96 of them, and some block holds exactly 96.
All inputs are finite; a program needn't handle non-finite values.
Results may differ from a plain program's by a relative error of at most 0.019.
Values may be sent and summed in bfloat16 or wider, within the bound.
A program may use at most 64 MiB of HBM per device.

v0:
```python
import jax
import jax.numpy as jnp
from jax import lax
from jax.sharding import PartitionSpec as P

GRID = 16


def joined_along(blocks, dim):
    dims = list(blocks.shape[1:])
    dims[dim] *= blocks.shape[0]
    return jnp.moveaxis(blocks, 0, dim).reshape(dims)


def work_in_pieces(shard, axis, dim, work, out_dim):
    span = shard.shape[dim]
    pieces = jnp.split(shard, 2, axis=dim) if span % 2 == 0 else [shard]
    first = jnp.arange(lax.axis_size(axis)) * span
    blocks = [lax.all_gather(slab, axis) for slab in pieces]
    made = [jax.vmap(work)(b, first + k * (span // len(pieces))) for k, b in enumerate(blocks)]
    return joined_along(jnp.concatenate(made, axis=out_dim + 1), out_dim)


def split_up(shard, dim, size):
    before, after = (shard.shape[:dim], shard.shape[dim + 1 :])
    return jnp.moveaxis(shard.reshape(*before, size, -1, *after), dim, 0)


def summed_on_arrival(shard, axis, dim):
    size = lax.axis_size(axis)
    blocks = lax.all_to_all(split_up(shard, dim, size), axis, 0, 0, tiled=True)
    return jnp.sum(blocks.astype(jnp.float32), axis=0)


def spline_basis(frac):
    remain = 1.0 - frac
    square = frac * frac
    cubed = square * frac
    values = (
        jnp.stack(
            [
                remain * remain * remain,
                3.0 * cubed - 6.0 * square + 4.0,
                -3.0 * cubed + 3.0 * square + 3.0 * frac + 1.0,
                cubed,
            ]
        )
        / 6.0
    )
    curves = jnp.stack([remain, 3.0 * frac - 2.0, 1.0 - 3.0 * frac, frac])
    return (values, curves)


def evaluate(coefficients, cell_one, frac_one, edge):
    shifts = jnp.arange(4, dtype=jnp.int32)[:, None] - 1
    index_x = (cell_one[0][None, :] + shifts) % edge
    index_y = (cell_one[1][None, :] + shifts) % edge
    index_z = (cell_one[2][None, :] + shifts) % edge
    value_x, curve_x = spline_basis(frac_one[0])
    value_y, curve_y = spline_basis(frac_one[1])
    value_z, curve_z = spline_basis(frac_one[2])
    plane = (index_y[:, None, :] * edge + index_z[None, :, :]).reshape(16, -1)
    value_yz = (value_y[:, None, :] * value_z[None, :, :]).reshape(16, -1)
    curve_yz = (
        curve_y[:, None, :] * value_z[None, :, :] + value_y[:, None, :] * curve_z[None, :, :]
    ).reshape(16, -1)
    electrons = cell_one.shape[1]
    orb_width = coefficients.shape[1]
    all_rows = (index_x[:, None, :] * (edge * edge) + plane[None, :, :]).reshape(64, electrons)
    weight_val = (value_x[:, None, :] * value_yz[None, :, :]).reshape(64, electrons)
    weight_lap = (
        curve_x[:, None, :] * value_yz[None, :, :] + value_x[:, None, :] * curve_yz[None, :, :]
    ).reshape(64, electrons)
    val_high = weight_val.astype(jnp.bfloat16)
    val_low = (weight_val - val_high.astype(jnp.float32)).astype(jnp.bfloat16)
    lap_high = weight_lap.astype(jnp.bfloat16)
    lap_low = (weight_lap - lap_high.astype(jnp.float32)).astype(jnp.bfloat16)
    stacked = jnp.stack([val_high, val_low, lap_high, lap_low])
    block = 256
    count = electrons // block
    rows_blocked = jnp.transpose(all_rows.reshape(64, count, block), (1, 2, 0))
    weights_blocked = jnp.transpose(stacked.reshape(4, 64, count, block), (2, 3, 0, 1))

    def one_block(items):
        rows_one, weights_one = items
        gathered = jnp.take(coefficients, rows_one, axis=0)
        parts = jnp.einsum(
            "nqk,nkw->nqw", weights_one, gathered, preferred_element_type=jnp.float32
        )
        orbital_sum = parts[:, 0, :] + parts[:, 1, :]
        laplace_sum = parts[:, 2, :] + parts[:, 3, :]
        return jnp.concatenate(
            [orbital_sum.astype(jnp.bfloat16), laplace_sum.astype(jnp.bfloat16)], axis=1
        )

    results = lax.map(one_block, (rows_blocked, weights_blocked))
    return results.reshape(electrons, 2 * orb_width)


def apply_inverse(inverse_rows, both_vals):

    def multiply(inv_piece, first_row):
        return jnp.dot(inv_piece, both_vals, preferred_element_type=jnp.float32)

    return work_in_pieces(inverse_rows, "orb", 0, multiply, 0)


def slot_tables(occupied, shard_index, orb_width, capacity):
    mine = occupied // orb_width == shard_index
    ranking = jnp.cumsum(mine.astype(jnp.int32)) - 1
    slot_ids = jnp.arange(capacity, dtype=jnp.int32)
    placed = mine[None, :] & (ranking[None, :] == slot_ids[:, None])
    positions = jnp.arange(occupied.shape[0], dtype=jnp.int32)
    slot_rows = jnp.sum(jnp.where(placed, positions[None, :], 0), axis=1)
    local_cols = occupied - shard_index * orb_width
    slot_cols = jnp.sum(jnp.where(placed, local_cols[None, :], 0), axis=1)
    filled = jnp.any(placed, axis=1)
    picker = (
        (jnp.arange(orb_width, dtype=jnp.int32)[:, None] == slot_cols[None, :]) & filled[None, :]
    ).astype(jnp.bfloat16)
    return (picker, slot_rows)


def couple_slots(kinetic_low, ratio, picker, slot_rows):
    slot_block = jnp.einsum(
        "ls,nl->sn", picker, kinetic_low, preferred_element_type=jnp.float32
    ).astype(jnp.bfloat16)
    ratio_rows = jnp.take(ratio, lax.all_gather(slot_rows, "orb", axis=0, tiled=True), axis=0)
    return jnp.einsum(
        "sn,sw->nw",
        lax.all_gather(slot_block, "orb", axis=0, tiled=True),
        ratio_rows,
        preferred_element_type=jnp.float32,
    )


def body(coefficients, inverse, cell_index, fraction, energies, weights, occupied):
    orb_width = coefficients.shape[1]
    orb_count = lax.axis_size("orb")
    shard_index = lax.axis_index("orb")
    electrons = occupied.shape[0]
    capacity = 3 * electrons // (2 * orb_count)
    picker, slot_rows = slot_tables(occupied, shard_index, orb_width, capacity)
    running = jnp.zeros((electrons, orb_width), jnp.float32)

    def finish(running, products, energy, weight):
        ratio = products[:, :orb_width].astype(jnp.bfloat16)
        kinetic = products[:, orb_width:]
        kinetic_low = kinetic.astype(jnp.bfloat16)
        coupled = couple_slots(kinetic_low, ratio, picker, slot_rows)
        sample_term = weight * (energy * ratio.astype(jnp.float32) - 0.5 * (kinetic - coupled))
        return running + sample_term

    def step_each(running, items):
        inverse_one, cells_one, frac_one, energy, weight = items
        products = apply_inverse(inverse_one, evaluate(coefficients, cells_one, frac_one, GRID))
        return (finish(running, products, energy, weight), None)

    running, unused = lax.scan(
        step_each, running, (inverse, cell_index, fraction, energies, weights)
    )
    return summed_on_arrival(running.astype(jnp.bfloat16), "walk", 0)


def solution(mesh):
    in_specs = (
        P(None, "orb"),
        P("walk", "orb", None),
        P("walk", None, None),
        P("walk", None, None),
        P("walk"),
        P("walk"),
        P(),
    )
    out_specs = P("walk", "orb")
    return jax.shard_map(body, mesh=mesh, in_specs=in_specs, out_specs=out_specs, check_vma=False)
```

profile of v0, /device:TPU:0, one launch (start us, length us, event | category | flops | bytes accessed | tf_op | source)
XLA Modules:
  0.0 392.6 jit_solution(9786935563459408953)
XLA Ops:
  6.5 1.7 fusion.39
  8.3 0.7 all-gather.4.cloned.1.call-update
  9.0 0.8 fusion.28
  9.8 0.8 broadcast_subtract_fusion.3
  10.9 0.1 add.378
  11.1 0.1 mul.535
  11.7 0.5 maximum_bitcast_fusion.1
  12.2 294.5 %while.17 = (s32[]{:T(128)}, bf16[4,256,512]{2,1,0:T(8,128)(2,1)}, bf16[4,256,4,64]{1,0,3,2:T(4,128)(2,1)S(1)}, s32[4,256,64]{1,0,2:T(4,128)S(1)}, bf16[4096,256]{1,0:T(8,128)(2,1)S(1)}, /*index=5*/s32[]{:T(128)}) while((s32[]{:T(128)}, bf16[4,256,512]{2,1,0:T(8,128)(2,1)}, bf16[4,256,4,64]{1,0,3,2:T(4,128)(2,1)S(1)}, ...), condition=%wide.region_1.2_spmd, body=%wide.region_0.1_spmd.sunk | while | flops 38699008 | bytes 30048844 | solution.py:96
  12.5 64.8 %gather_fusion = bf16[16384,256]{1,0:T(8,128)(2,1)} fusion(bf16[4096,256]{1,0:T(8,128)(2,1)S(1)} %get-tuple-element.202, s32[16384]{0:T(1024)S(1)} %broadcast_clamp_fusion.2), kind=kCustom, calls=%fused_computation.clone.1 | custom fusion | bytes 16842752 | tf_op jit(solution)/shard_map/while/body/eval_jaxpr/while/body/eval_jaxpr/jit(_take)/gather | solution.py:86
  77.4 0.3 constant_dynamic-slice_fusion.5
  77.7 0.2 copy.29
  77.9 6.5 %fusion.53 = f32[256,4,256]{2,1,0:T(4,128)S(1)} fusion(bf16[256,64,256]{2,1,0:T(8,128)(2,1)} %bitcast.100, pred[256,64]{1,0:T(8,128)(4,1)S(1)} %compare_and_fusion.3, bf16[1,256,4,64]{3,2,1,0:T(4,128)(2,1)S(1)} %copy.29), kind=kOutput, calls=%fused_computation.2.clone.1 | convolution fusion | flops 37748736 | bytes 9584640 | tf_op jit(solution)/shard_map/while/body/eval_jaxpr/while/body/eval_jaxpr/nqk,nkw->nqw/dot_general | solution.py:87
  84.3 0.7 fusion.54
  85.1 0.7 fusion.55
  86.1 64.8 %gather_fusion = bf16[16384,256]{1,0:T(8,128)(2,1)} fusion(bf16[4096,256]{1,0:T(8,128)(2,1)S(1)} %get-tuple-element.202, s32[16384]{0:T(1024)S(1)} %broadcast_clamp_fusion.2), kind=kCustom, calls=%fused_computation.clone.1 | custom fusion | bytes 16842752 | tf_op jit(solution)/shard_map/while/body/eval_jaxpr/while/body/eval_jaxpr/jit(_take)/gather | solution.py:86
  151.0 0.3 constant_dynamic-slice_fusion.5
  151.3 0.2 copy.29
  151.5 6.5 %fusion.53 = f32[256,4,256]{2,1,0:T(4,128)S(1)} fusion(bf16[256,64,256]{2,1,0:T(8,128)(2,1)} %bitcast.100, pred[256,64]{1,0:T(8,128)(4,1)S(1)} %compare_and_fusion.3, bf16[1,256,4,64]{3,2,1,0:T(4,128)(2,1)S(1)} %copy.29), kind=kOutput, calls=%fused_computation.2.clone.1 | convolution fusion | flops 37748736 | bytes 9584640 | tf_op jit(solution)/shard_map/while/body/eval_jaxpr/while/body/eval_jaxpr/nqk,nkw->nqw/dot_general | solution.py:87
  158.0 0.7 fusion.54
  158.7 0.7 fusion.55
  159.7 64.8 %gather_fusion = bf16[16384,256]{1,0:T(8,128)(2,1)} fusion(bf16[4096,256]{1,0:T(8,128)(2,1)S(1)} %get-tuple-element.202, s32[16384]{0:T(1024)S(1)} %broadcast_clamp_fusion.2), kind=kCustom, calls=%fused_computation.clone.1 | custom fusion | bytes 16842752 | tf_op jit(solution)/shard_map/while/body/eval_jaxpr/while/body/eval_jaxpr/jit(_take)/gather | solution.py:86
  224.6 0.3 constant_dynamic-slice_fusion.5
  224.9 0.2 copy.29
  225.1 6.5 %fusion.53 = f32[256,4,256]{2,1,0:T(4,128)S(1)} fusion(bf16[256,64,256]{2,1,0:T(8,128)(2,1)} %bitcast.100, pred[256,64]{1,0:T(8,128)(4,1)S(1)} %compare_and_fusion.3, bf16[1,256,4,64]{3,2,1,0:T(4,128)(2,1)S(1)} %copy.29), kind=kOutput, calls=%fused_computation.2.clone.1 | convolution fusion | flops 37748736 | bytes 9584640 | tf_op jit(solution)/shard_map/while/body/eval_jaxpr/while/body/eval_jaxpr/nqk,nkw->nqw/dot_general | solution.py:87
  231.6 0.7 fusion.54
  232.3 0.7 fusion.55
  233.3 64.8 %gather_fusion = bf16[16384,256]{1,0:T(8,128)(2,1)} fusion(bf16[4096,256]{1,0:T(8,128)(2,1)S(1)} %get-tuple-element.202, s32[16384]{0:T(1024)S(1)} %broadcast_clamp_fusion.2), kind=kCustom, calls=%fused_computation.clone.1 | custom fusion | bytes 16842752 | tf_op jit(solution)/shard_map/while/body/eval_jaxpr/while/body/eval_jaxpr/jit(_take)/gather | solution.py:86
  298.2 0.3 constant_dynamic-slice_fusion.5
  298.5 0.2 copy.29
  298.7 6.5 %fusion.53 = f32[256,4,256]{2,1,0:T(4,128)S(1)} fusion(bf16[256,64,256]{2,1,0:T(8,128)(2,1)} %bitcast.100, pred[256,64]{1,0:T(8,128)(4,1)S(1)} %compare_and_fusion.3, bf16[1,256,4,64]{3,2,1,0:T(4,128)(2,1)S(1)} %copy.29), kind=kOutput, calls=%fused_computation.2.clone.1 | convolution fusion | flops 37748736 | bytes 9584640 | tf_op jit(solution)/shard_map/while/body/eval_jaxpr/while/body/eval_jaxpr/nqk,nkw->nqw/dot_general | solution.py:87
  305.2 0.7 fusion.54
  305.9 0.7 fusion.55
  306.7 0.3 reduce-window.9
  307.2 0.2 fusion.17
  307.4 0.2 select_reduce_fusion
  307.6 2.2 convolution_bitcast_fusion
  309.9 2.2 convolution_bitcast_fusion.1
  312.2 0.2 pad_maximum_fusion
  312.4 1.3 convolution_convert_fusion
  315.0 0.6 dynamic-slice
  316.3 0.3 dynamic-update-slice
  316.5 15.5 %all-reduce = s32[1536]{0:T(1024)S(1)} all-reduce(s32[1536]{0:T(1024)S(1)} %dynamic-update-slice), channel_id=1, replica_groups=mesh['walk'=8,'orb'=16] {'orb'}, use_global_device_ids=true, to_apply=%add | all-reduce | flops 1536 | bytes 12288
  332.1 1.3 slice.118
  333.4 4.8 %gather_fusion.1 = bf16[1536,256]{1,0:T(8,128)(2,1)S(1)} fusion(bf16[1024,256]{1,0:T(8,128)(2,1)S(1)} %slice.118, s32[2048]{0:T(1024)S(1)} %pad_clamp_fusion), kind=kCustom, calls=%fused_computation.1 | custom fusion | bytes 1579008 | tf_op jit(solution)/shard_map/while/body/eval_jaxpr/jit(_take)/gather | solution.py:128
  338.2 28.8 %all-gather.8.cloned.1.call-done = bf16[1536,1024]{1,0:T(8,128)(2,1)} async-done(((bf16[96,1024]{1,0:T(8,128)(2,1)}), bf16[1536,1024]{1,0:T(8,128)(2,1)}) %all-gather.8.cloned.1.call-update) | async-done | bytes 3145744 | tf_op jit(solution)/shard_map/while/body/eval_jaxpr/all_gather | solution.py:131
  367.0 3.8 fusion.12
  370.8 14.6 %all_to_all.5 = bf16[8,128,256]{2,1,0:T(8,128)(2,1)S(1)} all-to-all(bf16[8,128,256]{2,1,0:T(8,128)(2,1)S(1)} %bitcast.105), channel_id=1, replica_groups=mesh['walk'=8,'orb'=16] {'walk'}, dimensions={0} | all-to-all | bytes 1048576 | tf_op jit(solution)/shard_map/all_to_all | solution.py:31
  385.3 0.7 convert_reduce_fusion
  (72 shorter events, 2.6 us)
Async XLA Ops:
  6.5 4.8 %copy-start.3 = (s32[1,3,1024]{2,0,1:T(1,128)S(1)}, s32[1,3,1024]{2,0,1:T(1,128)}, u32[]{:S(2)}) copy-start(s32[1,3,1024]{2,0,1:T(1,128)} %param.11) | copy-start | bytes 36868
  6.5 5.6 %copy-start = (bf16[4096,256]{1,0:T(8,128)(2,1)S(1)}, bf16[4096,256]{1,0:T(8,128)(2,1)}, u32[]{:S(2)}) copy-start(bf16[4096,256]{1,0:T(8,128)(2,1)} %param.9) | copy-start | bytes 6291460
  6.5 301.1 %all-gather.6.cloned.1.call-start = ((), (), s32[]{:S(2)}) async-start(), calls=%async_computation.2 | async-start | bytes 1114112 | tf_op jit(solution)/shard_map/while/body/eval_jaxpr/all_gather | solution.py:19
  8.2 301.7 %all-gather.4.cloned.1.call-start = ((), (), s32[]{:S(2)}) async-start(), calls=%async_computation.1 | async-start | bytes 1114112 | tf_op jit(solution)/shard_map/while/body/eval_jaxpr/all_gather | solution.py:19
  9.0 358.0 %all-gather.8.cloned.1.call-start = ((), (), s32[]{:S(2)}) async-start(), calls=%async_computation.3 | async-start | bytes 3342336 | tf_op jit(solution)/shard_map/while/body/eval_jaxpr/all_gather | solution.py:131
  12.2 294.5 %copy-start.2 = (s32[1024]{0:T(1024)S(1)}, s32[1024]{0:T(1024)}, u32[]{:S(2)}) copy-start(s32[1024]{0:T(1024)} %param.15) | copy-start | bytes 12292
  312.1 2.9 copy-start.4
  312.4 19.7 %copy-start.1 = (f32[16,64,512]{2,1,0:T(8,128)}, f32[16,64,512]{2,1,0:T(8,128)S(1)}, u32[]{:S(2)}) copy-start(f32[16,64,512]{2,1,0:T(8,128)S(1)} %pad_maximum_fusion) | copy-start | bytes 6291460
Sparse Core Ops, SparseCore 0:
  9.8 47.2 all-gather.5
  59.6 43.6 all-gather.3
  313.8 53.1 all-gather.7
where the time goes:
time: 393 us
  local copies, waits for them, and re-layouts  272 us (69%)
  matrix products  35.4 us (9%)
  blocking collectives  30.1 us (8%)
  waiting for transfers between devices  29.6 us (8%)
  between operations  15.4 us (4%)
  other arithmetic  10.2 us (3%)
    gather x4, local copies, waits for them, and re-layouts, one_block(): gathered = jnp.take(coefficients, rows_one, axis=0)  259 us
    all_gather x1, waiting for transfers between devices, couple_slots(): lax.all_gather(slot_block, 'orb', axis=0, tiled=True)  28.8 us
    dot_general x4, matrix products, one_block(): jnp.einsum('nqk,nkw->nqw', weights_one, gathered, preferred_element_type=...  25.9 us
    unnamed x1, blocking collectives  15.5 us
    all_to_all x1, blocking collectives, summed_on_arrival(): blocks = lax.all_to_all(split_up(shard, dim, size), axis, 0, 0, tiled=True)  14.6 us
  transfers between devices with their start and end apart: 3, of which 1 were waited for; matrix products, arithmetic and copies ran while one was open for 78% of the time, Pallas kernels for 0%

commit v1 on v0

--- a/solution.py
+++ b/solution.py
@@ -128,7 +128,9 @@
     ratio_rows = jnp.take(ratio, lax.all_gather(slot_rows, "orb", axis=0, tiled=True), axis=0)
     return jnp.einsum(
         "sn,sw->nw",
-        lax.all_gather(slot_block, "orb", axis=0, tiled=True),
+        jnp.concatenate(
+            lax.all_to_all(jnp.stack([slot_block] * lax.axis_size("orb")), "orb", 0, 0), axis=0
+        ),
         ratio_rows,
         preferred_element_type=jnp.float32,
     )

time: 393 us -> 406 us (1.033)
  waiting for transfers between devices: 29.6 us -> 0.74 us
  blocking collectives: 30.1 us -> 56.1 us
  starting transfers between devices: 0.08 us -> 8.21 us
    all_gather x1 -> x0, waiting for transfers between devices: 28.8 us -> none  [couple_slots(): lax.all_gather(slot_block, 'orb', axis=0, tiled=True)]
    unnamed x1, blocking collectives: 15.5 us -> 43.2 us
    all_to_all x0 -> x1, starting transfers between devices: none -> 8.17 us  [couple_slots(): lax.all_to_all(jnp.stack([slot_block] * lax.axis_size('orb')), 'orb', 0, 0)]
  transfers between devices with their start and end apart: 3 -> 3, of which waited for: 1 -> 0; matrix products, arithmetic and copies ran while one was open for 78% -> 77% of each run, Pallas kernels for 0% -> 0%
where the time goes in v1:
time: 406 us; the launch traced here: 402 us
  local copies, waits for them, and re-layouts  274 us (67%)
  blocking collectives  56.1 us (14%)
  matrix products  34.9 us (9%)
  between operations  15.6 us (4%)
  other arithmetic  12.5 us (3%)
  starting transfers between devices  8.21 us (2%)
    gather x4, local copies, waits for them, and re-layouts, one_block(): gathered = jnp.take(coefficients, rows_one, axis=0)  261 us
    unnamed x1, blocking collectives  43.2 us
    dot_general x4, matrix products, one_block(): jnp.einsum('nqk,nkw->nqw', weights_one, gathered, preferred_element_type=...  25.9 us
    all_to_all x1, blocking collectives, summed_on_arrival(): blocks = lax.all_to_all(split_up(shard, dim, size), axis, 0, 0, tiled=True)  13 us
    all_to_all x1, starting transfers between devices, couple_slots(): lax.all_to_all(jnp.stack([slot_block] * lax.axis_size('orb')), 'orb', 0, 0)  8.17 us
  transfers between devices with their start and end apart: 3, of which 0 were waited for; matrix products, arithmetic and copies ran while one was open for 77% of the time, Pallas kernels for 0%

profile of v1, /device:TPU:0, one launch (start us, length us, event | category | flops | bytes accessed | tf_op | source)
XLA Modules:
  0.0 402.3 jit_solution(5807631359581433649)
XLA Ops:
  6.5 1.7 fusion.39
  8.3 0.7 all-gather.3.cloned.1.call-update
  9.0 0.8 fusion.28
  9.8 0.8 broadcast_subtract_fusion.3
  11.0 0.7 subtract_convert_fusion
  11.9 0.8 subtract_convert_fusion.1
  13.0 1.5 maximum_bitcast_fusion.1
  14.5 295.9 %while.17 = (s32[]{:T(128)}, bf16[4,256,512]{2,1,0:T(8,128)(2,1)}, bf16[4,256,4,64]{1,0,3,2:T(4,128)(2,1)S(1)}, s32[4,256,64]{1,0,2:T(4,128)S(1)}, bf16[4096,256]{1,0:T(8,128)(2,1)S(1)}, /*index=5*/s32[]{:T(128)}) while((s32[]{:T(128)}, bf16[4,256,512]{2,1,0:T(8,128)(2,1)}, bf16[4,256,4,64]{1,0,3,2:T(4,128)(2,1)S(1)}, ...), condition=%wide.region_1.2_spmd, body=%wide.region_0.1_spmd.sunk | while | flops 38699008 | bytes 30048844 | solution.py:96
  14.8 65.2 %gather_fusion = bf16[16384,256]{1,0:T(8,128)(2,1)} fusion(bf16[4096,256]{1,0:T(8,128)(2,1)S(1)} %get-tuple-element.202, s32[16384]{0:T(1024)S(1)} %broadcast_clamp_fusion.2), kind=kCustom, calls=%fused_computation.clone.1 | custom fusion | bytes 16842752 | tf_op jit(solution)/shard_map/while/body/eval_jaxpr/while/body/eval_jaxpr/jit(_take)/gather | solution.py:86
  80.1 0.3 constant_dynamic-slice_fusion.5
  80.3 0.2 copy.29
  80.6 6.5 %fusion.53 = f32[256,4,256]{2,1,0:T(4,128)S(1)} fusion(bf16[256,64,256]{2,1,0:T(8,128)(2,1)} %bitcast.101, pred[256,64]{1,0:T(8,128)(4,1)S(1)} %compare_and_fusion.3, bf16[1,256,4,64]{3,2,1,0:T(4,128)(2,1)S(1)} %copy.29), kind=kOutput, calls=%fused_computation.2.clone.1 | convolution fusion | flops 37748736 | bytes 9584640 | tf_op jit(solution)/shard_map/while/body/eval_jaxpr/while/body/eval_jaxpr/nqk,nkw->nqw/dot_general | solution.py:87
  87.0 0.7 fusion.54
  87.8 0.7 fusion.55
  88.8 65.2 %gather_fusion = bf16[16384,256]{1,0:T(8,128)(2,1)} fusion(bf16[4096,256]{1,0:T(8,128)(2,1)S(1)} %get-tuple-element.202, s32[16384]{0:T(1024)S(1)} %broadcast_clamp_fusion.2), kind=kCustom, calls=%fused_computation.clone.1 | custom fusion | bytes 16842752 | tf_op jit(solution)/shard_map/while/body/eval_jaxpr/while/body/eval_jaxpr/jit(_take)/gather | solution.py:86
  154.0 0.3 constant_dynamic-slice_fusion.5
  154.3 0.2 copy.29
  154.5 6.5 %fusion.53 = f32[256,4,256]{2,1,0:T(4,128)S(1)} fusion(bf16[256,64,256]{2,1,0:T(8,128)(2,1)} %bitcast.101, pred[256,64]{1,0:T(8,128)(4,1)S(1)} %compare_and_fusion.3, bf16[1,256,4,64]{3,2,1,0:T(4,128)(2,1)S(1)} %copy.29), kind=kOutput, calls=%fused_computation.2.clone.1 | convolution fusion | flops 37748736 | bytes 9584640 | tf_op jit(solution)/shard_map/while/body/eval_jaxpr/while/body/eval_jaxpr/nqk,nkw->nqw/dot_general | solution.py:87
  161.0 0.7 fusion.54
  161.7 0.7 fusion.55
  162.8 65.2 %gather_fusion = bf16[16384,256]{1,0:T(8,128)(2,1)} fusion(bf16[4096,256]{1,0:T(8,128)(2,1)S(1)} %get-tuple-element.202, s32[16384]{0:T(1024)S(1)} %broadcast_clamp_fusion.2), kind=kCustom, calls=%fused_computation.clone.1 | custom fusion | bytes 16842752 | tf_op jit(solution)/shard_map/while/body/eval_jaxpr/while/body/eval_jaxpr/jit(_take)/gather | solution.py:86
  228.0 0.3 constant_dynamic-slice_fusion.5
  228.3 0.2 copy.29
  228.5 6.5 %fusion.53 = f32[256,4,256]{2,1,0:T(4,128)S(1)} fusion(bf16[256,64,256]{2,1,0:T(8,128)(2,1)} %bitcast.101, pred[256,64]{1,0:T(8,128)(4,1)S(1)} %compare_and_fusion.3, bf16[1,256,4,64]{3,2,1,0:T(4,128)(2,1)S(1)} %copy.29), kind=kOutput, calls=%fused_computation.2.clone.1 | convolution fusion | flops 37748736 | bytes 9584640 | tf_op jit(solution)/shard_map/while/body/eval_jaxpr/while/body/eval_jaxpr/nqk,nkw->nqw/dot_general | solution.py:87
  235.0 0.7 fusion.54
  235.7 0.7 fusion.55
  236.8 65.2 %gather_fusion = bf16[16384,256]{1,0:T(8,128)(2,1)} fusion(bf16[4096,256]{1,0:T(8,128)(2,1)S(1)} %get-tuple-element.202, s32[16384]{0:T(1024)S(1)} %broadcast_clamp_fusion.2), kind=kCustom, calls=%fused_computation.clone.1 | custom fusion | bytes 16842752 | tf_op jit(solution)/shard_map/while/body/eval_jaxpr/while/body/eval_jaxpr/jit(_take)/gather | solution.py:86
  302.0 0.3 constant_dynamic-slice_fusion.5
  302.3 0.2 copy.29
  302.5 6.5 %fusion.53 = f32[256,4,256]{2,1,0:T(4,128)S(1)} fusion(bf16[256,64,256]{2,1,0:T(8,128)(2,1)} %bitcast.101, pred[256,64]{1,0:T(8,128)(4,1)S(1)} %compare_and_fusion.3, bf16[1,256,4,64]{3,2,1,0:T(4,128)(2,1)S(1)} %copy.29), kind=kOutput, calls=%fused_computation.2.clone.1 | convolution fusion | flops 37748736 | bytes 9584640 | tf_op jit(solution)/shard_map/while/body/eval_jaxpr/while/body/eval_jaxpr/nqk,nkw->nqw/dot_general | solution.py:87
  309.0 0.7 fusion.54
  309.7 0.7 fusion.55
  310.4 0.3 reduce-window.9
  311.0 0.2 fusion.17
  311.2 0.2 select_reduce_fusion
  311.4 3.2 convolution_bitcast_fusion
  314.6 2.3 convolution_bitcast_fusion.1
  317.0 0.2 pad_maximum_fusion
  317.2 0.3 convolution_convert_fusion
  317.5 2.1 stack.142
  319.6 8.2 %all-to-all-start = ((bf16[16,96,1024]{2,1,0:T(8,128)(2,1)}), bf16[16,96,1024]{2,1,0:T(8,128)(2,1)}, u32[]{:S(2)}, u32[]{:S(2)}) async-start(bf16[16,96,1024]{2,1,0:T(8,128)(2,1)} %stack.142), calls=%async_computation | async-start | bytes 6291456 | tf_op jit(solution)/shard_map/while/body/eval_jaxpr/all_to_all | solution.py:132
  329.0 0.6 dynamic-slice
  330.3 0.3 dynamic-update-slice
  330.6 43.2 %all-reduce = s32[1536]{0:T(1024)S(1)} all-reduce(s32[1536]{0:T(1024)S(1)} %dynamic-update-slice), channel_id=1, replica_groups=mesh['walk'=8,'orb'=16] {'orb'}, use_global_device_ids=true, to_apply=%add | all-reduce | flops 1536 | bytes 12288
  373.8 4.8 %gather_fusion.1 = bf16[1536,256]{1,0:T(8,128)(2,1)S(1)} fusion(bf16[1024,256]{1,0:T(8,128)(2,1)S(1)} %slice.118, s32[2048]{0:T(1024)S(1)} %pad_clamp_fusion), kind=kCustom, calls=%fused_computation.1 | custom fusion | bytes 1579008 | tf_op jit(solution)/shard_map/while/body/eval_jaxpr/jit(_take)/gather | solution.py:128
  378.6 3.2 fusion.12
  381.8 13.0 %all_to_all.11 = bf16[8,128,256]{2,1,0:T(8,128)(2,1)S(1)} all-to-all(bf16[8,128,256]{2,1,0:T(8,128)(2,1)S(1)} %bitcast.106), channel_id=1, replica_groups=mesh['walk'=8,'orb'=16] {'walk'}, dimensions={0} | all-to-all | bytes 1048576 | tf_op jit(solution)/shard_map/all_to_all | solution.py:31
  394.7 0.7 convert_reduce_fusion
  (72 shorter events, 2.7 us)
Async XLA Ops:
  6.5 6.1 %copy-start.3 = (s32[1,3,1024]{2,0,1:T(1,128)S(1)}, s32[1,3,1024]{2,0,1:T(1,128)}, u32[]{:S(2)}) copy-start(s32[1,3,1024]{2,0,1:T(1,128)} %param.11) | copy-start | bytes 36868
  6.5 7.9 %copy-start = (bf16[4096,256]{1,0:T(8,128)(2,1)S(1)}, bf16[4096,256]{1,0:T(8,128)(2,1)}, u32[]{:S(2)}) copy-start(bf16[4096,256]{1,0:T(8,128)(2,1)} %param.9) | copy-start | bytes 6291460
  6.5 304.9 %all-gather.5.cloned.1.call-start = ((), (), s32[]{:S(2)}) async-start(), calls=%async_computation.3 | async-start | bytes 1114112 | tf_op jit(solution)/shard_map/while/body/eval_jaxpr/all_gather | solution.py:19
  8.2 306.4 %all-gather.3.cloned.1.call-start = ((), (), s32[]{:S(2)}) async-start(), calls=%async_computation.2 | async-start | bytes 1114112 | tf_op jit(solution)/shard_map/while/body/eval_jaxpr/all_gather | solution.py:19
  14.5 295.9 %copy-start.2 = (s32[1024]{0:T(1024)S(1)}, s32[1024]{0:T(1024)}, u32[]{:S(2)}) copy-start(s32[1024]{0:T(1024)} %param.15) | copy-start | bytes 12292
  314.6 2.3 copy-start.1
  319.6 9.5 %copy-start.4 = (u32[128]{0:T(128)S(1)}, u32[128]{0:T(128)}, u32[]{:S(2)}) copy-start(u32[128]{0:T(128)} %constant.157) | copy-start | bytes 1540
  319.6 59.0 %all-to-all-start = ((bf16[16,96,1024]{2,1,0:T(8,128)(2,1)}), bf16[16,96,1024]{2,1,0:T(8,128)(2,1)}, u32[]{:S(2)}, u32[]{:S(2)}) async-start(bf16[16,96,1024]{2,1,0:T(8,128)(2,1)} %stack.142), calls=%async_computation | async-start | bytes 6291456 | tf_op jit(solution)/shard_map/while/body/eval_jaxpr/all_to_all | solution.py:132
Sparse Core Ops, SparseCore 0:
  9.8 47.2 all-gather.4
  59.6 43.6 all-gather.2
